TPU v7x, 32 devices: a whole 2x2x4 slice. The times are simulated.
32 devices in a mesh: seq: 8 (over z, core), tp: 4 (over y, x).
Axes of the slice: x: 2, y: 2, z: 4, core: 2. Of those that a mesh axis runs over, the one named last changes fastest.
Arguments:
- queries: bfloat16 [8192, 4096], P(('seq', 'tp')), may hold values from -170 to 170, as said below
- keys: bfloat16 [8192, 512], P(('seq', 'tp')), may hold values from -6 to 6
- values: bfloat16 [8192, 512], P(('seq', 'tp')), may hold values from -6 to 6
- segments: int32 [8192], replicated, may hold values from 0 to 63, never falling along the last dimension, each value on 1 to 256 neighbouring positions
- out_weight: bfloat16 [4096, 4096], P('tp'), may hold values from -0.75 to 0.75
Outputs:
- mixed: bfloat16 [8192, 4096], P(('seq', 'tp'))
Inputs may be any that keep to these rules, and one draw needn't show every extreme that they name: `segments`: document ids never fall along the positions; one document holds at most 256 positions. `queries`: independent entries.
All inputs are finite; a program needn't handle non-finite values.
Results may differ from a plain program's by a relative error of at most 0.014.
Values may be sent and summed in bfloat16 or wider, within the bound.
A program may use at most 64 MiB of HBM per device.

v0:
```python
import functools

import jax
import jax.numpy as jnp
from jax import lax
from jax.experimental import pallas as pl
from jax.experimental.pallas import tpu as pltpu
from jax.sharding import PartitionSpec as P

KVH = 4
HD = 128
DOC = 256
TILE = DOC // 2


def from_behind(value, axis, steps):
    count = lax.axis_size(axis)
    first, last = (max(0, -steps), min(count, count - steps))
    return lax.ppermute(value, axis, [(source, source + steps) for source in range(first, last)])


def spread_heads(source, copies):
    if copies == 1:
        return source
    rows = source.shape[0]
    widened = jnp.repeat(source.reshape(rows, KVH, HD), copies, axis=1)
    return widened.reshape(rows, KVH * copies * HD)


def general_shards(queries, keys, values, segments, out_weight):
    tp_count = lax.axis_size("tp")
    copies = max(tp_count // KVH, 1)
    tile_rows = DOC // 2
    inverse_root = HD ** (-0.5)
    keys_wide = spread_heads(keys, copies)
    values_wide = spread_heads(values, copies)
    local_queries, local_keys, local_values = (
        lax.all_to_all(queries, "tp", split_axis=1, concat_axis=0, tiled=True),
        lax.all_to_all(keys_wide, "tp", split_axis=1, concat_axis=0, tiled=True),
        lax.all_to_all(values_wide, "tp", split_axis=1, concat_axis=0, tiled=True),
    )
    row_count = local_queries.shape[0]
    kv_local = local_keys.shape[1] // HD
    query_local = local_queries.shape[1] // HD
    local_group = query_local // kv_local
    tile_count = row_count // tile_rows
    first_row = lax.axis_index("seq") * row_count
    closing = jnp.stack([local_keys[row_count - DOC :], local_values[row_count - DOC :]])
    earlier = from_behind(closing, "seq", 1)
    key_ext = jnp.concatenate([earlier[0], local_keys], 0).reshape(row_count + DOC, kv_local, HD)
    value_ext = jnp.concatenate([earlier[1], local_values], 0).reshape(
        row_count + DOC, kv_local, HD
    )
    padded_seg = jnp.concatenate([jnp.full((DOC,), -1, jnp.int32), segments], 0)
    key_seg = lax.dynamic_slice_in_dim(padded_seg, first_row, row_count + DOC)
    query_seg = key_seg[DOC:].reshape(tile_count, tile_rows)
    key_pos = first_row - DOC + jnp.arange(row_count + DOC, dtype=jnp.int32)
    query_pos = (first_row + jnp.arange(row_count, dtype=jnp.int32)).reshape(tile_count, tile_rows)

    def windows(source):
        blocks = source.reshape((tile_count + 2, tile_rows) + source.shape[1:])
        return jnp.concatenate([blocks[:-2], blocks[1:-1], blocks[2:]], 1)

    key_win = windows(key_ext)
    value_win = windows(value_ext)
    pos_win = windows(key_pos)
    seg_win = windows(key_seg)
    query_tiles = local_queries.reshape(tile_count, tile_rows, kv_local, local_group, HD)
    allowed = (pos_win[:, None, :] <= query_pos[:, :, None]) & (
        seg_win[:, None, :] == query_seg[:, :, None]
    )
    allowed = allowed[:, None, None]
    scores = (
        jnp.einsum("ctkgd,cskd->ckgts", query_tiles, key_win, preferred_element_type=jnp.float32)
        * inverse_root
    )
    masked = jnp.where(allowed, scores, jnp.float32(-1e30))
    top_score = jnp.max(masked, axis=-1, keepdims=True)
    weights = jnp.where(allowed, jnp.exp(masked - top_score), jnp.float32(0.0))
    denominator = jnp.sum(weights, axis=-1)
    totals = jnp.einsum(
        "ckgts,cskd->ckgtd",
        weights.astype(jnp.bfloat16),
        value_win,
        preferred_element_type=jnp.float32,
    )
    attended = (totals / denominator[..., None]).astype(jnp.bfloat16)
    attended = jnp.transpose(attended, (0, 3, 1, 2, 4)).reshape(row_count, query_local * HD)
    return lax.psum_scatter(
        jnp.dot(attended, out_weight, preferred_element_type=jnp.float32).astype(jnp.bfloat16),
        "tp",
        scatter_dimension=0,
        tiled=True,
    )


PAIRS = 8


def kernel(
    n_seq,
    q_hbm,
    k_hbm,
    v_hbm,
    seg_ref,
    w_hbm,
    out_ref,
    qbuf,
    kwin,
    vwin,
    w_ref,
    w_side,
    att,
    bias,
    part,
    own,
    arrived,
    local_sem,
    in_send,
    in_recv,
    before_send,
    before_recv,
    w_send,
    w_recv,
    out_send,
    out_recv,
):
    rows, width = qbuf.shape[1], qbuf.shape[2]
    pair_width = kwin.shape[2]
    group = width // pair_width
    depth, n_out = w_ref.shape
    pair_cols = n_out // PAIRS
    chunk = pair_cols // 2
    half = depth // 2
    s = lax.axis_index("seq")
    me = lax.axis_index("tp")
    x = me % 2
    y = me // 2
    xn = y * 2 + 1 - x
    yn = (1 - y) * 2 + x
    core = s % 2
    parity = (s // 2) % 2
    peer = s + 1 - 2 * core
    plane = s + 2 - 4 * parity
    blocks = (me, yn)
    f32, bf16 = jnp.float32, jnp.bfloat16

    def cols(index, size):
        return pl.ds(pl.multiple_of(index * size, size), size)

    late = pl.ds(rows, rows)
    early = pl.ds(0, rows)
    locals_ = [
        pltpu.make_async_copy(k_hbm.at[:, cols(y, pair_width)], kwin.at[0, late], local_sem.at[0]),
        pltpu.make_async_copy(v_hbm.at[:, cols(y, pair_width)], vwin.at[0, late], local_sem.at[1]),
        pltpu.make_async_copy(q_hbm.at[:, cols(y, width)], qbuf.at[0], local_sem.at[2]),
        pltpu.make_async_copy(w_hbm, w_ref, local_sem.at[3]),
    ]
    for copy in locals_:
        copy.start()

    barrier = pltpu.get_barrier_semaphore()
    for target in ({"tp": xn}, {"tp": yn}, {"seq": peer}, {"seq": plane}):
        pl.semaphore_signal(barrier, inc=1, device_id=target)
    to_next = jnp.logical_and(x == 1, s < n_seq - 1)
    from_last = jnp.logical_and(x == 0, s > 0)

    @pl.when(to_next)
    def _():
        pl.semaphore_signal(barrier, inc=1, device_id={"seq": s + 1, "tp": xn})

    @pl.when(from_last)
    def _():
        pl.semaphore_signal(barrier, inc=1, device_id={"seq": s - 1, "tp": xn})

    pl.semaphore_wait(barrier, 4 + jnp.where(to_next, 1, 0) + jnp.where(from_last, 1, 0))

    def across(which):
        src, dst, size = (
            (k_hbm, kwin.at[1, late], pair_width),
            (v_hbm, vwin.at[1, late], pair_width),
        )[which]
        return pltpu.make_async_remote_copy(
            src_ref=src.at[:, cols(1 - y, size)],
            dst_ref=dst,
            send_sem=in_send.at[which],
            recv_sem=in_recv.at[which],
            device_id={"tp": yn},
        )

    def across_q(t, g):
        at = pl.ds(t * TILE, TILE)
        part_width = width // 2
        return pltpu.make_async_remote_copy(
            src_ref=q_hbm.at[at, cols((1 - y) * 2 + g, part_width)],
            dst_ref=qbuf.at[1, at, pl.ds(g * part_width, part_width)],
            send_sem=in_send.at[2 + 2 * t + g],
            recv_sem=in_recv.at[2 + 2 * t + g],
            device_id={"tp": yn},
        )

    def before(j, which, hop):
        win = (kwin, vwin)[which]
        src = (k_hbm, v_hbm)[which].at[:, cols(y, pair_width)] if j == 0 else win.at[1, late]
        slot = j + x * (1 - 2 * j)
        return pltpu.make_async_remote_copy(
            src_ref=src,
            dst_ref=win.at[slot, early],
            send_sem=before_send.at[which, j],
            recv_sem=before_recv.at[which, slot],
            device_id={"seq": lax.rem(s + hop, n_seq), "tp": xn},
        )

    def send_before(j):
        @pl.when(blocks[j] != 3)
        def _():
            before(j, 0, 0).start()
            before(j, 1, 0).start()

        @pl.when(jnp.logical_and(blocks[j] == 3, s < n_seq - 1))
        def _():
            before(j, 0, 1).start()
            before(j, 1, 1).start()

    def sent_before(j):
        @pl.when(jnp.logical_or(blocks[j] != 3, s < n_seq - 1))
        def _():
            before(j, 0, 0).wait_send()
            before(j, 1, 0).wait_send()

    def wait_before(j):
        @pl.when(jnp.logical_or(blocks[j] != 0, s > 0))
        def _():
            for which, win in enumerate((kwin, vwin)):
                pltpu.make_async_remote_copy(
                    src_ref=win.at[j, early],
                    dst_ref=win.at[j, early],
                    send_sem=before_send.at[which, j],
                    recv_sem=before_recv.at[which, j],
                    device_id={"tp": xn},
                ).wait_recv()

    mine = pl.ds(pl.multiple_of(core * half, half), half)

    def weight(i, stage):
        which = 1 - parity if stage == 3 else parity
        at = cols(2 * i + which, chunk)
        return pltpu.make_async_remote_copy(
            src_ref=(w_hbm if stage == 0 else w_side).at[mine, at],
            dst_ref=w_side.at[mine, at],
            send_sem=w_send.at[stage, i],
            recv_sem=w_recv.at[stage, i],
            device_id=({"tp": xn}, {"seq": plane}, {"seq": peer}, {"seq": peer})[stage],
        )

    def relay_direct(i):
        weight(i, 0).wait_recv()
        weight(i, 1).start()
        weight(i, 2).start()

    def relay_plane(i):
        weight(i, 1).wait_recv()
        weight(i, 3).start()

    across(0).start()
    across(1).start()
    tiles = rows // TILE
    for t in range(tiles):
        across_q(t, 0).start()
        across_q(t, 1).start()
    send_before(0)
    weight(0, 0).start()

    for j in range(2):

        @pl.when(jnp.logical_and(blocks[j] == 0, s == 0))
        def _():
            kwin[j, 0:rows] = jnp.zeros((rows, pair_width), bf16)
            vwin[j, 0:rows] = jnp.zeros((rows, pair_width), bf16)

    across(0).wait_recv()
    across(1).wait_recv()
    send_before(1)
    for i in range(1, PAIRS):
        weight(i, 0).start()
    for copy in locals_:
        copy.wait()

    causal_q = lax.broadcasted_iota(jnp.int32, (TILE, TILE), 0)
    causal_k = lax.broadcasted_iota(jnp.int32, (TILE, TILE), 1)

    def attend(j, t):
        row = (s * 4 + blocks[j]) * tiles + t

        def seg_row(at):
            got = seg_ref[pl.ds(jnp.maximum(at, 0), 1), :]
            return jnp.broadcast_to(jnp.where(at >= 0, got, -1), (TILE, TILE))

        current = seg_row(row)
        down = jnp.transpose(current)
        low, zero = f32(-1e30), f32(0.0)
        bias[:, 0:TILE] = jnp.where(seg_row(row - 2) == down, zero, low)
        bias[:, TILE : 2 * TILE] = jnp.where(seg_row(row - 1) == down, zero, low)
        bias[:, 2 * TILE : 3 * TILE] = jnp.where(
            jnp.logical_and(current == down, causal_k <= causal_q), zero, low
        )
        here = pl.ds(pl.multiple_of(t * TILE, TILE), TILE)
        window = pl.ds(pl.multiple_of(t * TILE, TILE), 3 * TILE)
        heads = width // HD
        for h in range(heads):
            if j == 1 and h % (heads // 2) == 0:
                across_q(t, h // (heads // 2)).wait_recv()
            span = slice(h * HD, (h + 1) * HD)
            kv = slice(h // group * HD, (h // group + 1) * HD)
            scores = lax.dot_general(
                qbuf[j, here, span],
                kwin[j, window, kv],
                (((1,), (1,)), ((), ())),
                preferred_element_type=f32,
            )
            scores = scores * (HD**-0.5) + bias[...]
            weights = jnp.exp(scores - jnp.max(scores, axis=-1, keepdims=True))
            denom = jnp.sum(weights, axis=-1, keepdims=True)
            total = jnp.dot(weights.astype(bf16), vwin[j, window, kv], preferred_element_type=f32)
            att[j, here, span] = (total / denom).astype(bf16)

    wait_before(0)

    @pl.loop(0, tiles)
    def _(t):
        attend(0, t)

    relay_direct(0)
    wait_before(1)
    attend(1, 0)
    relay_direct(1)
    relay_plane(0)
    for t in range(1, tiles):
        attend(1, t)
    relay_direct(2)

    def product(j, at):
        return jnp.dot(
            att[j, :, cols(x, depth)], w_ref[:, at], preferred_element_type=f32
        ) + jnp.dot(att[j, :, cols(1 - x, depth)], w_side[:, at], preferred_element_type=f32)

    def outward(i):
        at = cols(i, pair_cols)
        return pltpu.make_async_remote_copy(
            src_ref=part.at[:, at],
            dst_ref=arrived.at[:, at],
            send_sem=out_send.at[i],
            recv_sem=out_recv.at[i],
            device_id={"tp": yn},
        )

    @pl.loop(0, PAIRS)
    def _(i):
        weight(i, 2).wait_recv()
        weight(i, 3).wait_recv()
        at = cols(i, pair_cols)
        part[:, at] = product(1, at).astype(bf16)
        outward(i).start()
        own[:, at] = product(0, at)

        @pl.when(i + 1 < PAIRS)
        def _():
            relay_plane(i + 1)

        @pl.when(i + 3 < PAIRS)
        def _():
            relay_direct(i + 3)

    @pl.loop(0, PAIRS)
    def _(i):
        at = cols(i, pair_cols)
        outward(i).wait_recv()
        out_ref[:, at] = (own[:, at] + arrived[:, at].astype(f32)).astype(bf16)

    across(0).wait_send()
    across(1).wait_send()
    for t in range(tiles):
        across_q(t, 0).wait_send()
        across_q(t, 1).wait_send()
    sent_before(0)
    sent_before(1)

    @pl.loop(0, PAIRS)
    def _(i):
        for stage in range(4):
            weight(i, stage).wait_send()
        outward(i).wait_send()


def square_shards(n_seq, queries, keys, values, segments, out_weight):
    rows, n_q = queries.shape
    width = n_q // 2
    pair_width = keys.shape[1] // 2
    depth, n_out = out_weight.shape
    bf16 = jnp.bfloat16
    hbm = pl.BlockSpec(memory_space=pltpu.HBM)
    vmem = pl.BlockSpec(memory_space=pltpu.VMEM)
    dma = pltpu.SemaphoreType.DMA
    return pl.pallas_call(
        functools.partial(kernel, n_seq),
        out_shape=jax.ShapeDtypeStruct((rows, n_out), bf16),
        in_specs=[hbm, hbm, hbm, vmem, hbm],
        out_specs=vmem,
        scratch_shapes=[
            pltpu.VMEM((2, rows, width), bf16),
            pltpu.VMEM((2, 2 * rows, pair_width), bf16),
            pltpu.VMEM((2, 2 * rows, pair_width), bf16),
            pltpu.VMEM((depth, n_out), bf16),
            pltpu.VMEM((depth, n_out), bf16),
            pltpu.VMEM((2, rows, width), bf16),
            pltpu.VMEM((TILE, 3 * TILE), jnp.float32),
            pltpu.VMEM((rows, n_out), bf16),
            pltpu.VMEM((rows, n_out), jnp.float32),
            pltpu.VMEM((rows, n_out), bf16),
            dma((4,)),
            dma((2 + 2 * rows // TILE,)),
            dma((2 + 2 * rows // TILE,)),
            dma((2, 2)),
            dma((2, 2)),
            dma((4, PAIRS)),
            dma((4, PAIRS)),
            dma((PAIRS,)),
            dma((PAIRS,)),
        ],
        compiler_params=pltpu.CompilerParams(
            collective_id=0, has_side_effects=True, vmem_limit_bytes=50 * 1024 * 1024
        ),
    )(queries, keys, values, segments.reshape(-1, TILE), out_weight)


def solution(mesh):
    placed = (
        P(("seq", "tp"), None),
        P(("seq", "tp"), None),
        P(("seq", "tp"), None),
        P(),
        P("tp", None),
    )
    n_seq, n_tp = mesh.shape["seq"], mesh.shape["tp"]

    def shards(queries, keys, values, segments, out_weight):
        one_head_each = keys.shape[1] == n_tp * HD
        fits = n_tp == 4 and n_seq % 4 == 0 and queries.shape[0] == DOC
        if fits and one_head_each:
            return square_shards(n_seq, queries, keys, values, segments, out_weight)
        return general_shards(queries, keys, values, segments, out_weight)

    return jax.shard_map(
        shards, mesh=mesh, in_specs=placed, out_specs=P(("seq", "tp"), None), check_vma=False
    )
```

profile of v0, /device:TPU:0, one launch (start us, length us, event | category | flops | bytes accessed | tf_op | source)
XLA Modules:
  0.0 97.0 jit_solution(1278067819053809631)
XLA Ops:
  0.0 0.0 copy-start
  0.0 0.9 copy-done
  1.0 0.0 copy-start.1
  1.0 0.9 copy-done.1
  1.9 0.0 copy-start.2
  1.9 0.8 copy-done.2
  2.7 93.0 %shard_map.55 = bf16[256,4096]{1,0:T(8,128)(2,1)S(1)} custom-call(bf16[256,4096]{1,0:T(8,128)(2,1)} %q_hbm.1, bf16[256,512]{1,0:T(8,128)(2,1)S(1)} %copy-done, bf16[256,512]{1,0:T(8,128)(2,1)S(1)} %copy-done.1, s32[64,128]{1,0:T(8,128)S(1)} %bitcast.1, bf16[1024,4096]{1,0:T(8,128)(2,1)} %w_hbm.1), custom_call_target="tpu_custom_call" | custom-call | tf_op jit(solution)/shard_map/pallas_call | solution.py:404
  95.7 1.3 %copy.7 = bf16[256,4096]{1,0:T(8,128)(2,1)} copy(bf16[256,4096]{1,0:T(8,128)(2,1)S(1)} %shard_map.55) | data formatting | bytes 4194304
Async XLA Ops:
  0.0 0.9 copy-start
  1.0 0.9 copy-start.1
  1.9 0.8 copy-start.2
where the time goes:
time: 97.2 us; the launch traced here: 97 us
  Pallas kernels  93 us (96%)
  local copies, waits for them, and re-layouts  3.98 us (4%)
    pallas_call x1, Pallas kernels, square_shards(): pl.pallas_call(functools.partial(kernel, n_seq), out_shape=jax.ShapeDtype...  93 us
    unnamed x7, local copies, waits for them, and re-layouts  3.98 us

commit v1 on v0

--- a/solution.py
+++ b/solution.py
@@ -94,7 +94,10 @@
     )
 
 
-PAIRS = 8
+PAIRS = 16
+FIRST = 3
+SECOND = 5
+EARLY = 4
 
 
 def kernel(
@@ -102,9 +105,10 @@
     q_hbm,
     k_hbm,
     v_hbm,
-    seg_ref,
+    seg_hbm,
     w_hbm,
     out_ref,
+    seg_ref,
     qbuf,
     kwin,
     vwin,
@@ -155,6 +159,7 @@
         pltpu.make_async_copy(v_hbm.at[:, cols(y, pair_width)], vwin.at[0, late], local_sem.at[1]),
         pltpu.make_async_copy(q_hbm.at[:, cols(y, width)], qbuf.at[0], local_sem.at[2]),
         pltpu.make_async_copy(w_hbm, w_ref, local_sem.at[3]),
+        pltpu.make_async_copy(seg_hbm, seg_ref, local_sem.at[4]),
     ]
     for copy in locals_:
         copy.start()
@@ -268,8 +273,8 @@
     for t in range(tiles):
         across_q(t, 0).start()
         across_q(t, 1).start()
-    send_before(0)
-    weight(0, 0).start()
+    for i in range(FIRST):
+        weight(i, 0).start()
 
     for j in range(2):
 
@@ -278,38 +283,55 @@
             kwin[j, 0:rows] = jnp.zeros((rows, pair_width), bf16)
             vwin[j, 0:rows] = jnp.zeros((rows, pair_width), bf16)
 
+    def send_halo(urgent):
+        @pl.when(x == urgent)
+        def _():
+            send_before(0)
+
+        @pl.when(x != urgent)
+        def _():
+            send_before(1)
+
+    relay_direct(0)
     across(0).wait_recv()
     across(1).wait_recv()
-    send_before(1)
-    for i in range(1, PAIRS):
+    send_halo(1)
+    for i in range(FIRST, SECOND):
         weight(i, 0).start()
+    send_halo(0)
+
+    @pl.loop(SECOND, PAIRS)
+    def _(i):
+        weight(i, 0).start()
+
     for copy in locals_:
         copy.wait()
 
     causal_q = lax.broadcasted_iota(jnp.int32, (TILE, TILE), 0)
     causal_k = lax.broadcasted_iota(jnp.int32, (TILE, TILE), 1)
 
-    def attend(j, t):
+    def attend(j, t, part_of):
         row = (s * 4 + blocks[j]) * tiles + t
 
         def seg_row(at):
             got = seg_ref[pl.ds(jnp.maximum(at, 0), 1), :]
             return jnp.broadcast_to(jnp.where(at >= 0, got, -1), (TILE, TILE))
 
-        current = seg_row(row)
-        down = jnp.transpose(current)
-        low, zero = f32(-1e30), f32(0.0)
-        bias[:, 0:TILE] = jnp.where(seg_row(row - 2) == down, zero, low)
-        bias[:, TILE : 2 * TILE] = jnp.where(seg_row(row - 1) == down, zero, low)
-        bias[:, 2 * TILE : 3 * TILE] = jnp.where(
-            jnp.logical_and(current == down, causal_k <= causal_q), zero, low
-        )
-        here = pl.ds(pl.multiple_of(t * TILE, TILE), TILE)
-        window = pl.ds(pl.multiple_of(t * TILE, TILE), 3 * TILE)
+        if part_of == 0:
+            current = seg_row(row)
+            down = jnp.transpose(current)
+            low, zero = f32(-1e30), f32(0.0)
+            bias[:, 0:TILE] = jnp.where(seg_row(row - 2) == down, zero, low)
+            bias[:, TILE : 2 * TILE] = jnp.where(seg_row(row - 1) == down, zero, low)
+            bias[:, 2 * TILE : 3 * TILE] = jnp.where(
+                jnp.logical_and(current == down, causal_k <= causal_q), zero, low
+            )
+        here = pl.ds(t * TILE, TILE)
+        window = pl.ds(t * TILE, 3 * TILE)
         heads = width // HD
-        for h in range(heads):
-            if j == 1 and h % (heads // 2) == 0:
-                across_q(t, h // (heads // 2)).wait_recv()
+        if j == 1:
+            across_q(t, part_of).wait_recv()
+        for h in range(part_of * (heads // 2), (part_of + 1) * (heads // 2)):
             span = slice(h * HD, (h + 1) * HD)
             kv = slice(h // group * HD, (h // group + 1) * HD)
             scores = lax.dot_general(
@@ -324,57 +346,112 @@
             total = jnp.dot(weights.astype(bf16), vwin[j, window, kv], preferred_element_type=f32)
             att[j, here, span] = (total / denom).astype(bf16)
 
-    wait_before(0)
-
-    @pl.loop(0, tiles)
-    def _(t):
-        attend(0, t)
-
-    relay_direct(0)
-    wait_before(1)
-    attend(1, 0)
+    def product(j, at, here):
+        return jnp.dot(
+            att[j, here, cols(x, depth)], w_ref[:, at], preferred_element_type=f32
+        ) + jnp.dot(att[j, here, cols(1 - x, depth)], w_side[:, at], preferred_element_type=f32)
+
+    def outward(i, here, slot):
+        at = cols(i, pair_cols)
+        return pltpu.make_async_remote_copy(
+            src_ref=part.at[here, at],
+            dst_ref=arrived.at[here, at],
+            send_sem=out_send.at[slot, i],
+            recv_sem=out_recv.at[slot, i],
+            device_id={"tp": yn},
+        )
+
+    every = pl.ds(0, rows)
+    tile0, tile1 = pl.ds(0, TILE), pl.ds(TILE, TILE)
+
+    def whole(i):
+        weight(i, 2).wait_recv()
+        weight(i, 3).wait_recv()
+
+    def export(i, here, slot):
+        part[here, cols(i, pair_cols)] = product(1, cols(i, pair_cols), here).astype(bf16)
+        outward(i, here, slot).start()
+
+    def keep(i):
+        at = cols(i, 2 * pair_cols)
+        own[:, at] = product(0, at, every)
+
     relay_direct(1)
     relay_plane(0)
-    for t in range(1, tiles):
-        attend(1, t)
     relay_direct(2)
-
-    def product(j, at):
-        return jnp.dot(
-            att[j, :, cols(x, depth)], w_ref[:, at], preferred_element_type=f32
-        ) + jnp.dot(att[j, :, cols(1 - x, depth)], w_side[:, at], preferred_element_type=f32)
-
-    def outward(i):
+    wait_before(1)
+    attend(1, 0, 0)
+    relay_plane(1)
+    relay_plane(2)
+    attend(1, 0, 1)
+    relay_direct(3)
+    for i in range(3):
+        whole(i)
+        export(i, tile0, 0)
+    relay_direct(4)
+    relay_plane(3)
+    whole(3)
+    export(3, tile0, 0)
+    attend(1, 1, 0)
+    relay_plane(4)
+    relay_direct(5)
+    attend(1, 1, 1)
+    relay_direct(6)
+
+    @pl.loop(0, EARLY)
+    def _(i):
+        export(i, tile1, 1)
+
+    relay_plane(5)
+    whole(4)
+    export(4, every, 0)
+    wait_before(0)
+    attend(0, 0, 0)
+    relay_direct(7)
+    relay_plane(6)
+    relay_direct(8)
+    whole(5)
+    export(5, every, 0)
+    attend(0, 0, 1)
+    relay_plane(7)
+    relay_direct(9)
+    whole(6)
+    export(6, every, 0)
+    attend(0, 1, 0)
+    relay_plane(8)
+    relay_direct(10)
+    whole(7)
+    export(7, every, 0)
+    attend(0, 1, 1)
+    relay_plane(9)
+    relay_direct(11)
+
+    @pl.loop(8, PAIRS)
+    def _(i):
+        whole(i)
+        export(i, every, 0)
+
+        @pl.when(i + 2 < PAIRS)
+        def _():
+            relay_plane(i + 2)
+
+        @pl.when(i + 4 < PAIRS)
+        def _():
+            relay_direct(i + 4)
+
+        keep(i - 8)
+
+    @pl.loop(0, EARLY)
+    def _(i):
+        outward(i, tile0, 0).wait_recv()
+        outward(i, tile1, 1).wait_recv()
         at = cols(i, pair_cols)
-        return pltpu.make_async_remote_copy(
-            src_ref=part.at[:, at],
-            dst_ref=arrived.at[:, at],
-            send_sem=out_send.at[i],
-            recv_sem=out_recv.at[i],
-            device_id={"tp": yn},
-        )
-
-    @pl.loop(0, PAIRS)
-    def _(i):
-        weight(i, 2).wait_recv()
-        weight(i, 3).wait_recv()
+        out_ref[:, at] = (own[:, at] + arrived[:, at].astype(f32)).astype(bf16)
+
+    @pl.loop(EARLY, PAIRS)
+    def _(i):
+        outward(i, every, 0).wait_recv()
         at = cols(i, pair_cols)
-        part[:, at] = product(1, at).astype(bf16)
-        outward(i).start()
-        own[:, at] = product(0, at)
-
-        @pl.when(i + 1 < PAIRS)
-        def _():
-            relay_plane(i + 1)
-
-        @pl.when(i + 3 < PAIRS)
-        def _():
-            relay_direct(i + 3)
-
-    @pl.loop(0, PAIRS)
-    def _(i):
-        at = cols(i, pair_cols)
-        outward(i).wait_recv()
         out_ref[:, at] = (own[:, at] + arrived[:, at].astype(f32)).astype(bf16)
 
     across(0).wait_send()
@@ -389,7 +466,15 @@
     def _(i):
         for stage in range(4):
             weight(i, stage).wait_send()
-        outward(i).wait_send()
+
+    @pl.loop(0, EARLY)
+    def _(i):
+        outward(i, tile0, 0).wait_send()
+        outward(i, tile1, 1).wait_send()
+
+    @pl.loop(EARLY, PAIRS)
+    def _(i):
+        outward(i, every, 0).wait_send()
 
 
 def square_shards(n_seq, queries, keys, values, segments, out_weight):
@@ -404,9 +489,10 @@
     return pl.pallas_call(
         functools.partial(kernel, n_seq),
         out_shape=jax.ShapeDtypeStruct((rows, n_out), bf16),
-        in_specs=[hbm, hbm, hbm, vmem, hbm],
+        in_specs=[hbm, hbm, hbm, hbm, hbm],
         out_specs=vmem,
         scratch_shapes=[
+            pltpu.VMEM((segments.shape[0] // TILE, TILE), jnp.int32),
             pltpu.VMEM((2, rows, width), bf16),
             pltpu.VMEM((2, 2 * rows, pair_width), bf16),
             pltpu.VMEM((2, 2 * rows, pair_width), bf16),
@@ -417,20 +503,25 @@
             pltpu.VMEM((rows, n_out), bf16),
             pltpu.VMEM((rows, n_out), jnp.float32),
             pltpu.VMEM((rows, n_out), bf16),
-            dma((4,)),
+            dma((5,)),
             dma((2 + 2 * rows // TILE,)),
             dma((2 + 2 * rows // TILE,)),
             dma((2, 2)),
             dma((2, 2)),
             dma((4, PAIRS)),
             dma((4, PAIRS)),
-            dma((PAIRS,)),
-            dma((PAIRS,)),
+            dma((2, PAIRS)),
+            dma((2, PAIRS)),
         ],
         compiler_params=pltpu.CompilerParams(
             collective_id=0, has_side_effects=True, vmem_limit_bytes=50 * 1024 * 1024
         ),
-    )(queries, keys, values, segments.reshape(-1, TILE), out_weight)
+    )(
+        *(
+            pltpu.with_memory_space_constraint(a, pltpu.HBM)
+            for a in (queries, keys, values, segments.reshape(-1, TILE), out_weight)
+        )
+    )
 
 
 def solution(mesh):

time: 97.2 us -> 83.8 us (0.86)
  Pallas kernels: 93 us -> 82.3 us
  local copies, waits for them, and re-layouts: 3.98 us -> 1.32 us
    pallas_call x1, Pallas kernels: 93 us -> 82.3 us  [square_shards(): pl.pallas_call(functools.partial(kernel, n_seq), out_shape=jax.ShapeDtype...]
    unnamed x7 -> x1, local copies, waits for them, and re-layouts: 3.98 us -> 1.32 us
where the time goes in v1:
time: 83.8 us; the launch traced here: 83.7 us
  Pallas kernels  82.3 us (98%)
  local copies, waits for them, and re-layouts  1.32 us (2%)
    pallas_call x1, Pallas kernels, square_shards(): pl.pallas_call(functools.partial(kernel, n_seq), out_shape=jax.ShapeDtype...  82.3 us

profile of v1, /device:TPU:0, one launch (start us, length us, event | category | flops | bytes accessed | tf_op | source)
XLA Modules:
  0.0 83.7 jit_solution(11063495468895365800)
XLA Ops:
  0.0 82.3 %shard_map.55 = bf16[256,4096]{1,0:T(8,128)(2,1)S(1)} custom-call(bf16[256,4096]{1,0:T(8,128)(2,1)} %q_hbm.1, bf16[256,512]{1,0:T(8,128)(2,1)} %k_hbm.1, bf16[256,512]{1,0:T(8,128)(2,1)} %v_hbm.1, s32[64,128]{1,0:T(8,128)} %bitcast.1, bf16[1024,4096]{1,0:T(8,128)(2,1)} %w_hbm.1), custom_call_target="tpu_custom_call" | custom-call | tf_op jit(solution)/shard_map/pallas_call | solution.py:489
  82.4 1.3 %copy.7 = bf16[256,4096]{1,0:T(8,128)(2,1)} copy(bf16[256,4096]{1,0:T(8,128)(2,1)S(1)} %shard_map.55) | data formatting | bytes 4194304

commit v2 on v1

--- a/solution.py
+++ b/solution.py
@@ -97,7 +97,7 @@
 PAIRS = 16
 FIRST = 3
 SECOND = 5
-EARLY = 4
+EARLY = 5
 
 
 def kernel(
@@ -109,6 +109,7 @@
     w_hbm,
     out_ref,
     seg_ref,
+    kv_out,
     qbuf,
     kwin,
     vwin,
@@ -154,6 +155,16 @@
 
     late = pl.ds(rows, rows)
     early = pl.ds(0, rows)
+    early_ = [
+        pltpu.make_async_copy(
+            (k_hbm, v_hbm)[which].at[:, cols(1 - y, pair_width)],
+            kv_out.at[which],
+            local_sem.at[5 + which],
+        )
+        for which in range(2)
+    ]
+    for copy in early_:
+        copy.start()
     locals_ = [
         pltpu.make_async_copy(k_hbm.at[:, cols(y, pair_width)], kwin.at[0, late], local_sem.at[0]),
         pltpu.make_async_copy(v_hbm.at[:, cols(y, pair_width)], vwin.at[0, late], local_sem.at[1]),
@@ -181,13 +192,9 @@
     pl.semaphore_wait(barrier, 4 + jnp.where(to_next, 1, 0) + jnp.where(from_last, 1, 0))
 
     def across(which):
-        src, dst, size = (
-            (k_hbm, kwin.at[1, late], pair_width),
-            (v_hbm, vwin.at[1, late], pair_width),
-        )[which]
         return pltpu.make_async_remote_copy(
-            src_ref=src.at[:, cols(1 - y, size)],
-            dst_ref=dst,
+            src_ref=kv_out.at[which],
+            dst_ref=(kwin, vwin)[which].at[1, late],
             send_sem=in_send.at[which],
             recv_sem=in_recv.at[which],
             device_id={"tp": yn},
@@ -246,6 +253,7 @@
                 ).wait_recv()
 
     mine = pl.ds(pl.multiple_of(core * half, half), half)
+    theirs = pl.ds(pl.multiple_of((1 - core) * half, half), half)
 
     def weight(i, stage):
         which = 1 - parity if stage == 3 else parity
@@ -253,8 +261,8 @@
         return pltpu.make_async_remote_copy(
             src_ref=(w_hbm if stage == 0 else w_side).at[mine, at],
             dst_ref=w_side.at[mine, at],
-            send_sem=w_send.at[stage, i],
-            recv_sem=w_recv.at[stage, i],
+            send_sem=w_send.at[stage],
+            recv_sem=w_recv.at[min(stage, 2), i],
             device_id=({"tp": xn}, {"seq": plane}, {"seq": peer}, {"seq": peer})[stage],
         )
 
@@ -267,8 +275,9 @@
         weight(i, 1).wait_recv()
         weight(i, 3).start()
 
-    across(0).start()
-    across(1).start()
+    for which in range(2):
+        early_[which].wait()
+        across(which).start()
     tiles = rows // TILE
     for t in range(tiles):
         across_q(t, 0).start()
@@ -310,14 +319,14 @@
     causal_q = lax.broadcasted_iota(jnp.int32, (TILE, TILE), 0)
     causal_k = lax.broadcasted_iota(jnp.int32, (TILE, TILE), 1)
 
-    def attend(j, t, part_of):
+    def attend(j, t, quarter):
         row = (s * 4 + blocks[j]) * tiles + t
 
         def seg_row(at):
             got = seg_ref[pl.ds(jnp.maximum(at, 0), 1), :]
             return jnp.broadcast_to(jnp.where(at >= 0, got, -1), (TILE, TILE))
 
-        if part_of == 0:
+        if quarter == 0:
             current = seg_row(row)
             down = jnp.transpose(current)
             low, zero = f32(-1e30), f32(0.0)
@@ -329,9 +338,9 @@
         here = pl.ds(t * TILE, TILE)
         window = pl.ds(t * TILE, 3 * TILE)
         heads = width // HD
-        if j == 1:
-            across_q(t, part_of).wait_recv()
-        for h in range(part_of * (heads // 2), (part_of + 1) * (heads // 2)):
+        if j == 1 and quarter % 2 == 0:
+            across_q(t, quarter // 2).wait_recv()
+        for h in range(quarter * (heads // 4), (quarter + 1) * (heads // 4)):
             span = slice(h * HD, (h + 1) * HD)
             kv = slice(h // group * HD, (h // group + 1) * HD)
             scores = lax.dot_general(
@@ -351,13 +360,12 @@
             att[j, here, cols(x, depth)], w_ref[:, at], preferred_element_type=f32
         ) + jnp.dot(att[j, here, cols(1 - x, depth)], w_side[:, at], preferred_element_type=f32)
 
-    def outward(i, here, slot):
-        at = cols(i, pair_cols)
+    def outward(here, at, group):
         return pltpu.make_async_remote_copy(
             src_ref=part.at[here, at],
             dst_ref=arrived.at[here, at],
-            send_sem=out_send.at[slot, i],
-            recv_sem=out_recv.at[slot, i],
+            send_sem=out_send.at[0],
+            recv_sem=out_recv.at[group],
             device_id={"tp": yn},
         )
 
@@ -365,12 +373,19 @@
     tile0, tile1 = pl.ds(0, TILE), pl.ds(TILE, TILE)
 
     def whole(i):
-        weight(i, 2).wait_recv()
-        weight(i, 3).wait_recv()
-
-    def export(i, here, slot):
-        part[here, cols(i, pair_cols)] = product(1, cols(i, pair_cols), here).astype(bf16)
-        outward(i, here, slot).start()
+        held = w_side.at[theirs, cols(i, pair_cols)]
+        pltpu.make_async_remote_copy(
+            src_ref=held,
+            dst_ref=held,
+            send_sem=w_send.at[2],
+            recv_sem=w_recv.at[2, i],
+            device_id={"seq": peer},
+        ).wait_recv()
+
+    def export(i, here, group):
+        at = cols(i, pair_cols)
+        part[here, at] = product(1, at, here).astype(bf16)
+        outward(here, at, group).start()
 
     def keep(i):
         at = cols(i, 2 * pair_cols)
@@ -379,80 +394,97 @@
     relay_direct(1)
     relay_plane(0)
     relay_direct(2)
+    relay_plane(1)
     wait_before(1)
     attend(1, 0, 0)
-    relay_plane(1)
+    attend(1, 0, 1)
     relay_plane(2)
-    attend(1, 0, 1)
     relay_direct(3)
-    for i in range(3):
-        whole(i)
-        export(i, tile0, 0)
+    attend(1, 0, 2)
+    attend(1, 0, 3)
+    whole(0)
+    export(0, tile0, 0)
+    whole(1)
+    export(1, tile0, 0)
+    whole(2)
+    export(2, tile0, 0)
     relay_direct(4)
     relay_plane(3)
+    attend(1, 1, 0)
     whole(3)
     export(3, tile0, 0)
-    attend(1, 1, 0)
+    attend(1, 1, 1)
     relay_plane(4)
+    whole(4)
+    export(4, tile0, 0)
     relay_direct(5)
-    attend(1, 1, 1)
+    attend(1, 1, 2)
+    attend(1, 1, 3)
     relay_direct(6)
 
     @pl.loop(0, EARLY)
     def _(i):
-        export(i, tile1, 1)
-
-    relay_plane(5)
-    whole(4)
-    export(4, every, 0)
+        export(i, tile1, 0)
+
+    relay_direct(7)
     wait_before(0)
     attend(0, 0, 0)
-    relay_direct(7)
+    relay_plane(5)
+    relay_direct(8)
+    attend(0, 0, 1)
     relay_plane(6)
-    relay_direct(8)
     whole(5)
     export(5, every, 0)
-    attend(0, 0, 1)
+    relay_direct(9)
     relay_plane(7)
-    relay_direct(9)
     whole(6)
     export(6, every, 0)
-    attend(0, 1, 0)
+    attend(0, 0, 2)
+    relay_direct(10)
     relay_plane(8)
-    relay_direct(10)
     whole(7)
     export(7, every, 0)
+    attend(0, 0, 3)
+    relay_direct(11)
+    relay_plane(9)
+    whole(8)
+    export(8, every, 0)
+    attend(0, 1, 0)
+    relay_direct(12)
+    relay_plane(10)
+    whole(9)
+    export(9, every, 0)
     attend(0, 1, 1)
-    relay_plane(9)
-    relay_direct(11)
-
-    @pl.loop(8, PAIRS)
+    relay_direct(13)
+    relay_plane(11)
+    whole(10)
+    export(10, every, 0)
+    attend(0, 1, 2)
+    relay_direct(14)
+    relay_plane(12)
+    whole(11)
+    export(11, every, 0)
+    attend(0, 1, 3)
+    relay_direct(15)
+    relay_plane(13)
+    whole(12)
+    export(12, every, 0)
+    keep(0)
+    relay_plane(14)
+    whole(13)
+    export(13, every, 0)
+    keep(1)
+    relay_plane(15)
+    whole(14)
+    export(14, every, 1)
+    keep(2)
+    whole(15)
+    export(15, every, 2)
+
+    @pl.loop(3, 8)
     def _(i):
-        whole(i)
-        export(i, every, 0)
-
-        @pl.when(i + 2 < PAIRS)
-        def _():
-            relay_plane(i + 2)
-
-        @pl.when(i + 4 < PAIRS)
-        def _():
-            relay_direct(i + 4)
-
-        keep(i - 8)
-
-    @pl.loop(0, EARLY)
-    def _(i):
-        outward(i, tile0, 0).wait_recv()
-        outward(i, tile1, 1).wait_recv()
-        at = cols(i, pair_cols)
-        out_ref[:, at] = (own[:, at] + arrived[:, at].astype(f32)).astype(bf16)
-
-    @pl.loop(EARLY, PAIRS)
-    def _(i):
-        outward(i, every, 0).wait_recv()
-        at = cols(i, pair_cols)
-        out_ref[:, at] = (own[:, at] + arrived[:, at].astype(f32)).astype(bf16)
+        keep(i)
+
 
     across(0).wait_send()
     across(1).wait_send()
@@ -462,19 +494,30 @@
     sent_before(0)
     sent_before(1)
 
-    @pl.loop(0, PAIRS)
+    for stage in range(4):
+        sent = w_side.at[mine, pl.ds(0, n_out // 2)]
+        pltpu.make_async_remote_copy(
+            src_ref=sent,
+            dst_ref=sent,
+            send_sem=w_send.at[stage],
+            recv_sem=w_recv.at[0, 0],
+            device_id={"tp": xn},
+        ).wait_send()
+
+    def settle(at):
+        out_ref[:, at] = (own[:, at] + arrived[:, at].astype(f32)).astype(bf16)
+
+    outward(every, pl.ds(0, (PAIRS - 2) * pair_cols), 0).wait_recv()
+
+    @pl.loop(0, PAIRS // 2 - 1)
     def _(i):
-        for stage in range(4):
-            weight(i, stage).wait_send()
-
-    @pl.loop(0, EARLY)
-    def _(i):
-        outward(i, tile0, 0).wait_send()
-        outward(i, tile1, 1).wait_send()
-
-    @pl.loop(EARLY, PAIRS)
-    def _(i):
-        outward(i, every, 0).wait_send()
+        settle(cols(i, 2 * pair_cols))
+
+    for i in range(PAIRS - 2, PAIRS):
+        at = cols(i, pair_cols)
+        outward(every, at, i - PAIRS + 3).wait_recv()
+        settle(at)
+    outward(every, pl.ds(0, n_out), 0).wait_send()
 
 
 def square_shards(n_seq, queries, keys, values, segments, out_weight):
@@ -493,6 +536,7 @@
         out_specs=vmem,
         scratch_shapes=[
             pltpu.VMEM((segments.shape[0] // TILE, TILE), jnp.int32),
+            pltpu.VMEM((2, rows, pair_width), bf16),
             pltpu.VMEM((2, rows, width), bf16),
             pltpu.VMEM((2, 2 * rows, pair_width), bf16),
             pltpu.VMEM((2, 2 * rows, pair_width), bf16),
@@ -503,15 +547,15 @@
             pltpu.VMEM((rows, n_out), bf16),
             pltpu.VMEM((rows, n_out), jnp.float32),
             pltpu.VMEM((rows, n_out), bf16),
-            dma((5,)),
+            dma((7,)),
             dma((2 + 2 * rows // TILE,)),
             dma((2 + 2 * rows // TILE,)),
             dma((2, 2)),
             dma((2, 2)),
-            dma((4, PAIRS)),
-            dma((4, PAIRS)),
-            dma((2, PAIRS)),
-            dma((2, PAIRS)),
+            dma((4,)),
+            dma((3, PAIRS)),
+            dma((1,)),
+            dma((3,)),
         ],
         compiler_params=pltpu.CompilerParams(
             collective_id=0, has_side_effects=True, vmem_limit_bytes=50 * 1024 * 1024

time: 83.8 us -> 80.8 us (0.964)
  Pallas kernels: 82.3 us -> 79.3 us
    pallas_call x1, Pallas kernels: 82.3 us -> 79.3 us  [square_shards(): pl.pallas_call(functools.partial(kernel, n_seq), out_shape=jax.ShapeDtype...]
where the time goes in v2:
time: 80.8 us; the launch traced here: 80.6 us
  Pallas kernels  79.3 us (98%)
  local copies, waits for them, and re-layouts  1.32 us (2%)
    pallas_call x1, Pallas kernels, square_shards(): pl.pallas_call(functools.partial(kernel, n_seq), out_shape=jax.ShapeDtype...  79.3 us

profile of v2, /device:TPU:0, one launch (start us, length us, event | category | flops | bytes accessed | tf_op | source)
XLA Modules:
  0.0 80.6 jit_solution(3221371304688247406)
XLA Ops:
  0.0 79.3 %shard_map.55 = bf16[256,4096]{1,0:T(8,128)(2,1)S(1)} custom-call(bf16[256,4096]{1,0:T(8,128)(2,1)} %q_hbm.1, bf16[256,512]{1,0:T(8,128)(2,1)} %k_hbm.1, bf16[256,512]{1,0:T(8,128)(2,1)} %v_hbm.1, s32[64,128]{1,0:T(8,128)} %bitcast.1, bf16[1024,4096]{1,0:T(8,128)(2,1)} %w_hbm.1), custom_call_target="tpu_custom_call" | custom-call | tf_op jit(solution)/shard_map/pallas_call | solution.py:532
  79.3 1.3 %copy.7 = bf16[256,4096]{1,0:T(8,128)(2,1)} copy(bf16[256,4096]{1,0:T(8,128)(2,1)S(1)} %shard_map.55) | data formatting | bytes 4194304

commit v3 on v2

--- a/solution.py
+++ b/solution.py
@@ -129,6 +129,7 @@
     w_recv,
     out_send,
     out_recv,
+    entered,
 ):
     rows, width = qbuf.shape[1], qbuf.shape[2]
     pair_width = kwin.shape[2]
@@ -178,24 +179,30 @@
     barrier = pltpu.get_barrier_semaphore()
     for target in ({"tp": xn}, {"tp": yn}, {"seq": peer}, {"seq": plane}):
         pl.semaphore_signal(barrier, inc=1, device_id=target)
-    to_next = jnp.logical_and(x == 1, s < n_seq - 1)
-    from_last = jnp.logical_and(x == 0, s > 0)
-
-    @pl.when(to_next)
+    ahead = jnp.logical_and(x == 1, s < n_seq - 1)
+    behind = jnp.logical_and(x == 1, s > 0)
+    above = jnp.logical_and(ahead, core == 1)
+    below = jnp.logical_and(behind, core == 0)
+
+    @pl.when(above)
     def _():
-        pl.semaphore_signal(barrier, inc=1, device_id={"seq": s + 1, "tp": xn})
-
-    @pl.when(from_last)
+        pl.semaphore_signal(barrier, inc=1, device_id={"seq": s + 1})
+
+    @pl.when(below)
     def _():
-        pl.semaphore_signal(barrier, inc=1, device_id={"seq": s - 1, "tp": xn})
-
-    pl.semaphore_wait(barrier, 4 + jnp.where(to_next, 1, 0) + jnp.where(from_last, 1, 0))
+        pl.semaphore_signal(barrier, inc=1, device_id={"seq": s - 1})
+
+    pl.semaphore_wait(barrier, 4 + jnp.where(above, 1, 0) + jnp.where(below, 1, 0))
+
+    @pl.when(behind)
+    def _():
+        pl.semaphore_signal(entered, inc=1, device_id={"seq": s - 1})
 
     def across(which):
         return pltpu.make_async_remote_copy(
             src_ref=kv_out.at[which],
             dst_ref=(kwin, vwin)[which].at[1, late],
-            send_sem=in_send.at[which],
+            send_sem=in_send.at[0],
             recv_sem=in_recv.at[which],
             device_id={"tp": yn},
         )
@@ -206,7 +213,7 @@
         return pltpu.make_async_remote_copy(
             src_ref=q_hbm.at[at, cols((1 - y) * 2 + g, part_width)],
             dst_ref=qbuf.at[1, at, pl.ds(g * part_width, part_width)],
-            send_sem=in_send.at[2 + 2 * t + g],
+            send_sem=in_send.at[1],
             recv_sem=in_recv.at[2 + 2 * t + g],
             device_id={"tp": yn},
         )
@@ -218,7 +225,7 @@
         return pltpu.make_async_remote_copy(
             src_ref=src,
             dst_ref=win.at[slot, early],
-            send_sem=before_send.at[which, j],
+            send_sem=before_send.at[j],
             recv_sem=before_recv.at[which, slot],
             device_id={"seq": lax.rem(s + hop, n_seq), "tp": xn},
         )
@@ -234,11 +241,15 @@
             before(j, 0, 1).start()
             before(j, 1, 1).start()
 
+    def sent(src, sem):
+        pltpu.make_async_remote_copy(
+            src_ref=src, dst_ref=src, send_sem=sem, recv_sem=w_recv.at[0, 0], device_id={"tp": xn}
+        ).wait_send()
+
     def sent_before(j):
         @pl.when(jnp.logical_or(blocks[j] != 3, s < n_seq - 1))
         def _():
-            before(j, 0, 0).wait_send()
-            before(j, 1, 0).wait_send()
+            sent(kwin.at[j], before_send.at[j])
 
     def wait_before(j):
         @pl.when(jnp.logical_or(blocks[j] != 0, s > 0))
@@ -247,7 +258,7 @@
                 pltpu.make_async_remote_copy(
                     src_ref=win.at[j, early],
                     dst_ref=win.at[j, early],
-                    send_sem=before_send.at[which, j],
+                    send_sem=before_send.at[j],
                     recv_sem=before_recv.at[which, j],
                     device_id={"tp": xn},
                 ).wait_recv()
@@ -301,7 +312,10 @@
         def _():
             send_before(1)
 
-    relay_direct(0)
+    @pl.when(ahead)
+    def _():
+        pl.semaphore_wait(entered, 1)
+
     across(0).wait_recv()
     across(1).wait_recv()
     send_halo(1)
@@ -313,6 +327,7 @@
     def _(i):
         weight(i, 0).start()
 
+    relay_direct(0)
     for copy in locals_:
         copy.wait()
 
@@ -426,57 +441,57 @@
     def _(i):
         export(i, tile1, 0)
 
+    relay_plane(5)
     relay_direct(7)
+    whole(5)
+    export(5, every, 0)
     wait_before(0)
     attend(0, 0, 0)
-    relay_plane(5)
     relay_direct(8)
+    relay_plane(6)
     attend(0, 0, 1)
-    relay_plane(6)
-    whole(5)
-    export(5, every, 0)
+    whole(6)
+    export(6, every, 0)
     relay_direct(9)
     relay_plane(7)
-    whole(6)
-    export(6, every, 0)
     attend(0, 0, 2)
+    whole(7)
+    export(7, every, 0)
     relay_direct(10)
     relay_plane(8)
-    whole(7)
-    export(7, every, 0)
     attend(0, 0, 3)
+    whole(8)
+    export(8, every, 0)
     relay_direct(11)
     relay_plane(9)
-    whole(8)
-    export(8, every, 0)
     attend(0, 1, 0)
+    whole(9)
+    export(9, every, 0)
     relay_direct(12)
     relay_plane(10)
-    whole(9)
-    export(9, every, 0)
     attend(0, 1, 1)
+    whole(10)
+    export(10, every, 0)
     relay_direct(13)
     relay_plane(11)
-    whole(10)
-    export(10, every, 0)
     attend(0, 1, 2)
+    whole(11)
+    export(11, every, 0)
     relay_direct(14)
     relay_plane(12)
-    whole(11)
-    export(11, every, 0)
     attend(0, 1, 3)
+    whole(12)
+    export(12, every, 0)
     relay_direct(15)
     relay_plane(13)
-    whole(12)
-    export(12, every, 0)
     keep(0)
-    relay_plane(14)
     whole(13)
     export(13, every, 0)
+    relay_plane(14)
     keep(1)
-    relay_plane(15)
     whole(14)
     export(14, every, 1)
+    relay_plane(15)
     keep(2)
     whole(15)
     export(15, every, 2)
@@ -486,23 +501,13 @@
         keep(i)
 
 
-    across(0).wait_send()
-    across(1).wait_send()
-    for t in range(tiles):
-        across_q(t, 0).wait_send()
-        across_q(t, 1).wait_send()
+    sent(kv_out, in_send.at[0])
+    sent(qbuf.at[1], in_send.at[1])
     sent_before(0)
     sent_before(1)
 
     for stage in range(4):
-        sent = w_side.at[mine, pl.ds(0, n_out // 2)]
-        pltpu.make_async_remote_copy(
-            src_ref=sent,
-            dst_ref=sent,
-            send_sem=w_send.at[stage],
-            recv_sem=w_recv.at[0, 0],
-            device_id={"tp": xn},
-        ).wait_send()
+        sent(w_side.at[mine, pl.ds(0, n_out // 2)], w_send.at[stage])
 
     def settle(at):
         out_ref[:, at] = (own[:, at] + arrived[:, at].astype(f32)).astype(bf16)
@@ -548,14 +553,15 @@
             pltpu.VMEM((rows, n_out), jnp.float32),
             pltpu.VMEM((rows, n_out), bf16),
             dma((7,)),
+            dma((2,)),
             dma((2 + 2 * rows // TILE,)),
-            dma((2 + 2 * rows // TILE,)),
-            dma((2, 2)),
+            dma((2,)),
             dma((2, 2)),
             dma((4,)),
             dma((3, PAIRS)),
             dma((1,)),
             dma((3,)),
+            pltpu.SemaphoreType.REGULAR,
         ],
         compiler_params=pltpu.CompilerParams(
             collective_id=0, has_side_effects=True, vmem_limit_bytes=50 * 1024 * 1024

time: 80.8 us -> 80.6 us (level)
  no operation moved by 1% of the time
where the time goes in v3:
time: 80.6 us; the launch traced here: 80.4 us
  Pallas kernels  79.1 us (98%)
  local copies, waits for them, and re-layouts  1.32 us (2%)
    pallas_call x1, Pallas kernels, square_shards(): pl.pallas_call(functools.partial(kernel, n_seq), out_shape=jax.ShapeDtype...  79.1 us

profile of v3, /device:TPU:0, one launch (start us, length us, event | category | flops | bytes accessed | tf_op | source)
XLA Modules:
  0.0 80.4 jit_solution(454497194792762654)
XLA Ops:
  0.0 79.1 %shard_map.55 = bf16[256,4096]{1,0:T(8,128)(2,1)S(1)} custom-call(bf16[256,4096]{1,0:T(8,128)(2,1)} %q_hbm.1, bf16[256,512]{1,0:T(8,128)(2,1)} %k_hbm.1, bf16[256,512]{1,0:T(8,128)(2,1)} %v_hbm.1, s32[64,128]{1,0:T(8,128)} %bitcast.1, bf16[1024,4096]{1,0:T(8,128)(2,1)} %w_hbm.1), custom_call_target="tpu_custom_call" | custom-call | tf_op jit(solution)/shard_map/pallas_call | solution.py:537
  79.1 1.3 %copy.7 = bf16[256,4096]{1,0:T(8,128)(2,1)} copy(bf16[256,4096]{1,0:T(8,128)(2,1)S(1)} %shard_map.55) | data formatting | bytes 4194304

commit v4 on v3

--- a/solution.py
+++ b/solution.py
@@ -490,13 +490,37 @@
     relay_plane(14)
     keep(1)
     whole(14)
-    export(14, every, 1)
+
+    @pl.when(core == 0)
+    def _():
+        export(14, every, 1)
+
     relay_plane(15)
     keep(2)
     whole(15)
-    export(15, every, 2)
-
-    @pl.loop(3, 8)
+
+    @pl.when(core == 0)
+    def _():
+        export(15, every, 2)
+
+    keep(3)
+
+    @pl.when(core == 1)
+    def _():
+        export(14, every, 1)
+
+
+    @pl.loop(4, 6)
+    def _(i):
+        keep(i)
+
+
+    @pl.when(core == 1)
+    def _():
+        export(15, every, 2)
+
+
+    @pl.loop(6, 8)
     def _(i):
         keep(i)
 

time: 80.6 us -> 79.9 us (level); the launches traced: 80.4 us -> 78.8 us
  Pallas kernels: 79.1 us -> 77.5 us
    pallas_call x1, Pallas kernels: 79.1 us -> 77.5 us  [square_shards(): pl.pallas_call(functools.partial(kernel, n_seq), out_shape=jax.ShapeDtype...]
where the time goes in v4:
time: 79.9 us; the launch traced here: 78.8 us
  Pallas kernels  77.5 us (97%)
  local copies, waits for them, and re-layouts  1.32 us (2%)
    pallas_call x1, Pallas kernels, square_shards(): pl.pallas_call(functools.partial(kernel, n_seq), out_shape=jax.ShapeDtype...  77.5 us

profile of v4, /device:TPU:0, one launch (start us, length us, event | category | flops | bytes accessed | tf_op | source)
XLA Modules:
  0.0 78.8 jit_solution(8031071210098124408)
XLA Ops:
  0.0 77.5 %shard_map.55 = bf16[256,4096]{1,0:T(8,128)(2,1)S(1)} custom-call(bf16[256,4096]{1,0:T(8,128)(2,1)} %q_hbm.1, bf16[256,512]{1,0:T(8,128)(2,1)} %k_hbm.1, bf16[256,512]{1,0:T(8,128)(2,1)} %v_hbm.1, s32[64,128]{1,0:T(8,128)} %bitcast.1, bf16[1024,4096]{1,0:T(8,128)(2,1)} %w_hbm.1), custom_call_target="tpu_custom_call" | custom-call | tf_op jit(solution)/shard_map/pallas_call | solution.py:561
  77.5 1.3 %copy.7 = bf16[256,4096]{1,0:T(8,128)(2,1)} copy(bf16[256,4096]{1,0:T(8,128)(2,1)S(1)} %shard_map.55) | data formatting | bytes 4194304

commit v5 on v4

--- a/solution.py
+++ b/solution.py
@@ -156,6 +156,22 @@
 
     late = pl.ds(rows, rows)
     early = pl.ds(0, rows)
+    barrier = pltpu.get_barrier_semaphore()
+    for target in ({"tp": yn}, {"tp": xn}, {"seq": plane}, {"seq": peer}):
+        pl.semaphore_signal(barrier, inc=1, device_id=target)
+    ahead = jnp.logical_and(x == 1, s < n_seq - 1)
+    behind = jnp.logical_and(x == 1, s > 0)
+    above = jnp.logical_and(ahead, core == 1)
+    below = jnp.logical_and(behind, core == 0)
+
+    @pl.when(above)
+    def _():
+        pl.semaphore_signal(barrier, inc=1, device_id={"seq": s + 1})
+
+    @pl.when(below)
+    def _():
+        pl.semaphore_signal(barrier, inc=1, device_id={"seq": s - 1})
+
     early_ = [
         pltpu.make_async_copy(
             (k_hbm, v_hbm)[which].at[:, cols(1 - y, pair_width)],
@@ -175,22 +191,6 @@
     ]
     for copy in locals_:
         copy.start()
-
-    barrier = pltpu.get_barrier_semaphore()
-    for target in ({"tp": xn}, {"tp": yn}, {"seq": peer}, {"seq": plane}):
-        pl.semaphore_signal(barrier, inc=1, device_id=target)
-    ahead = jnp.logical_and(x == 1, s < n_seq - 1)
-    behind = jnp.logical_and(x == 1, s > 0)
-    above = jnp.logical_and(ahead, core == 1)
-    below = jnp.logical_and(behind, core == 0)
-
-    @pl.when(above)
-    def _():
-        pl.semaphore_signal(barrier, inc=1, device_id={"seq": s + 1})
-
-    @pl.when(below)
-    def _():
-        pl.semaphore_signal(barrier, inc=1, device_id={"seq": s - 1})
 
     pl.semaphore_wait(barrier, 4 + jnp.where(above, 1, 0) + jnp.where(below, 1, 0))
 

time: 79.9 us -> 79.9 us (level)
  no operation moved by 1% of the time
where the time goes in v5:
time: 79.9 us; the launch traced here: 78.8 us
  Pallas kernels  77.5 us (97%)
  local copies, waits for them, and re-layouts  1.32 us (2%)
    pallas_call x1, Pallas kernels, square_shards(): pl.pallas_call(functools.partial(kernel, n_seq), out_shape=jax.ShapeDtype...  77.5 us

profile of v5, /device:TPU:0, one launch (start us, length us, event | category | flops | bytes accessed | tf_op | source)
XLA Modules:
  0.0 78.8 jit_solution(3183240400720731279)
XLA Ops:
  0.0 77.5 %shard_map.55 = bf16[256,4096]{1,0:T(8,128)(2,1)S(1)} custom-call(bf16[256,4096]{1,0:T(8,128)(2,1)} %q_hbm.1, bf16[256,512]{1,0:T(8,128)(2,1)} %k_hbm.1, bf16[256,512]{1,0:T(8,128)(2,1)} %v_hbm.1, s32[64,128]{1,0:T(8,128)} %bitcast.1, bf16[1024,4096]{1,0:T(8,128)(2,1)} %w_hbm.1), custom_call_target="tpu_custom_call" | custom-call | tf_op jit(solution)/shard_map/pallas_call | solution.py:561
  77.5 1.3 %copy.7 = bf16[256,4096]{1,0:T(8,128)(2,1)} copy(bf16[256,4096]{1,0:T(8,128)(2,1)S(1)} %shard_map.55) | data formatting | bytes 4194304
